TPU v7x, 32 devices: a whole 2x2x4 slice. The times are simulated.
32 devices in a mesh: dp: 8 (over y, x, core), tensor: 4 (over z).
Axes of the slice: x: 2, y: 2, z: 4, core: 2. Of those that a mesh axis runs over, the one named last changes fastest.
Arguments:
- tokens: bfloat16 [16384, 768], P(('dp', 'tensor')), may hold values from -6 to 6
- segments: int32 [16384], P('dp'), may hold values from -1 to 9, as said below
- cotangent: bfloat16 [16384, 768], P(('dp', 'tensor')), may hold values from -6 to 6
- ln1_gain: bfloat16 [768], replicated, may hold values from 0.5 to 1.5
- ln1_bias: bfloat16 [768], replicated, may hold values from -2 to 2
- w_qkv: bfloat16 [768, 2304], P(None, 'tensor'), may hold values from -0.21875 to 0.21875
- q_bias: bfloat16 [768], P('tensor'), may hold values from -3 to 3
- v_bias: bfloat16 [768], P('tensor'), may hold values from -3 to 3
- w_out: bfloat16 [768, 768], P('tensor'), may hold values from -0.625 to 0.625
- out_bias: bfloat16 [768], replicated, may hold values from -2 to 2
- ln2_gain: bfloat16 [768], replicated, may hold values from 0.5 to 1.5
- ln2_bias: bfloat16 [768], replicated, may hold values from -2 to 2
- w_fc1: bfloat16 [768, 3072], P(None, 'tensor'), may hold values from -0.21875 to 0.21875
- fc1_bias: bfloat16 [3072], P('tensor'), may hold values from -3 to 3
- w_fc2: bfloat16 [3072, 768], P('tensor'), may hold values from -0.109375 to 0.109375
- fc2_bias: bfloat16 [768], replicated, may hold values from -2 to 2
Outputs:
- output: bfloat16 [16384, 768], P(('dp', 'tensor'))
- grad_tokens: bfloat16 [16384, 768], P(('dp', 'tensor'))
- cls_features: float32 [16384, 768], P(('dp', 'tensor'))
- grad_w_qkv: float32 [768, 2304], P('dp', 'tensor')
- grad_q_bias: float32 [768], replicated
- grad_v_bias: float32 [768], replicated
- grad_w_out: float32 [768, 768], P('tensor', 'dp')
- grad_out_bias: float32 [768], replicated
- grad_w_fc1: float32 [768, 3072], P('dp', 'tensor')
- grad_fc1_bias: float32 [3072], replicated
- grad_w_fc2: float32 [3072, 768], P('tensor', 'dp')
- grad_fc2_bias: float32 [768], replicated
- grad_ln1_gain: float32 [768], replicated
- grad_ln1_bias: float32 [768], replicated
- grad_ln2_gain: float32 [768], replicated
- grad_ln2_bias: float32 [768], replicated
Inputs may be any that keep to these rules, and one draw needn't show every extreme that they name: `segments`: within each aligned block of 512 positions the ids run 0, 1, 2, ... in order, id i over a run of 1 + 49 v positions with v from 1 to 4, starting at the block's first position; positions after the block's last whole sample hold -1. The first block begins with a run of 197; the last block holds only runs of 50, as many as fit.
All inputs are finite; a program needn't handle non-finite values.
Results may differ from a plain program's by a relative error of at most 0.024.
Values may be sent and summed in bfloat16 or wider, within the bound.
A program may use at most 128 MiB of HBM per device.

v0:
```python
from functools import partial
import math
import jax
import jax.numpy as jnp
from jax import lax
from jax.sharding import PartitionSpec as P

HD = 64
SEQ = 512


def layer_norm(values, gain, shift):
    average = jnp.mean(values, axis=-1, keepdims=True)
    centered = values - average
    spread = jnp.mean(centered * centered, axis=-1, keepdims=True)
    return centered * lax.rsqrt(spread + 1e-06) * gain + shift


def gelu_exact(values):
    return jax.nn.gelu(values, approximate=False)


def masked_scores(query_rows, key_rows, labels, score_scale):
    scores = (
        jnp.einsum("qhd,khd->hqk", query_rows, key_rows, preferred_element_type=jnp.float32)
        * score_scale
    )
    same_sample = labels[:, None] == labels[None, :]
    return jnp.where(same_sample[None], scores, -1e30)


def block_forward(inputs, score_scale):
    query_rows, key_rows, value_rows, labels = inputs
    scores = masked_scores(query_rows, key_rows, labels, score_scale)
    highest = jnp.max(scores, axis=-1, keepdims=True)
    expon = jnp.exp(scores - highest)
    totals = jnp.sum(expon, axis=-1, keepdims=True)
    weights = (expon / totals).astype(jnp.bfloat16)
    attended = jnp.einsum(
        "hqk,khd->qhd", weights, value_rows, preferred_element_type=jnp.float32
    ).astype(jnp.bfloat16)
    return (attended, (highest + jnp.log(totals))[..., 0])


def block_backward(inputs, score_scale):
    query_rows, key_rows, value_rows, labels, log_totals, grad_heads = inputs
    scores = masked_scores(query_rows, key_rows, labels, score_scale)
    weights = jnp.exp(scores - log_totals[..., None])
    grad_values = jnp.einsum(
        "hqk,qhd->khd", weights.astype(jnp.bfloat16), grad_heads, preferred_element_type=jnp.float32
    ).astype(jnp.bfloat16)
    grad_weights = jnp.einsum(
        "qhd,khd->hqk", grad_heads, value_rows, preferred_element_type=jnp.float32
    )
    inner = jnp.sum(grad_weights * weights, axis=-1, keepdims=True)
    grad_scores = (weights * (grad_weights - inner)).astype(jnp.bfloat16)
    grad_queries = (
        jnp.einsum("hqk,khd->qhd", grad_scores, key_rows, preferred_element_type=jnp.float32)
        * score_scale
    ).astype(jnp.bfloat16)
    grad_keys = (
        jnp.einsum("hqk,qhd->khd", grad_scores, query_rows, preferred_element_type=jnp.float32)
        * score_scale
    ).astype(jnp.bfloat16)
    return (grad_queries, grad_keys, grad_values)


def place_block(piece, tensor_index, tensor_parts):
    whole = jnp.zeros((piece.shape[0] * tensor_parts,), jnp.float32)
    return lax.dynamic_update_slice_in_dim(whole, piece, tensor_index * piece.shape[0], 0)


def on_device(
    tokens,
    segments,
    cotangent,
    ln1_gain,
    ln1_bias,
    w_qkv,
    q_bias,
    v_bias,
    w_out,
    out_bias,
    ln2_gain,
    ln2_bias,
    w_fc1,
    fc1_bias,
    w_fc2,
    fc2_bias,
):
    tensor_parts = lax.axis_size("tensor")
    tensor_index = lax.axis_index("tensor")
    rows_here = tokens.shape[0]
    all_rows = segments.shape[0]
    score_scale = 1.0 / math.sqrt(HD)
    positions = jnp.arange(all_rows) % SEQ
    earlier = jnp.concatenate([jnp.full((1,), -2, jnp.int32), segments[:-1]])
    first_all = ((segments >= 0) & ((positions == 0) | (segments != earlier))).astype(jnp.float32)
    first_rows = lax.dynamic_slice_in_dim(first_all, tensor_index * rows_here, rows_here)
    labels_here = lax.dynamic_slice_in_dim(segments, tensor_index * rows_here, rows_here)
    live_rows = (labels_here >= 0).astype(jnp.float32)
    inputs_f = tokens.astype(jnp.float32)
    normed, norm1_back = jax.vjp(
        layer_norm, inputs_f, ln1_gain.astype(jnp.float32), ln1_bias.astype(jnp.float32)
    )
    normed_low = normed.astype(jnp.bfloat16)
    weight_qkv, weight_out, bias_query, bias_value = (w_qkv, w_out, q_bias, v_bias)
    attn_source = lax.all_gather(normed_low, "tensor", axis=0, tiled=True)
    attn_total = attn_source.shape[0]
    block_count = attn_total // SEQ
    head_count = weight_qkv.shape[1] // (3 * HD)
    label_blocks = segments.reshape(block_count, SEQ)
    mixed = jnp.dot(attn_source, weight_qkv, preferred_element_type=jnp.float32).reshape(
        attn_total, head_count, 3, HD
    )
    query_rows = (mixed[:, :, 0] + bias_query.astype(jnp.float32).reshape(head_count, HD)).astype(
        jnp.bfloat16
    )
    key_rows = mixed[:, :, 1].astype(jnp.bfloat16)
    value_rows = (mixed[:, :, 2] + bias_value.astype(jnp.float32).reshape(head_count, HD)).astype(
        jnp.bfloat16
    )

    def blocked(array):
        return array.reshape(block_count, SEQ, head_count, HD)

    attended, log_totals = lax.map(
        partial(block_forward, score_scale=score_scale),
        (blocked(query_rows), blocked(key_rows), blocked(value_rows), label_blocks),
    )
    heads_out = attended.reshape(attn_total, head_count * HD)
    attn_sum = lax.psum_scatter(
        jnp.dot(heads_out, weight_out, preferred_element_type=jnp.float32).astype(jnp.bfloat16),
        "tensor",
        scatter_dimension=0,
        tiled=True,
    ).astype(jnp.float32)
    resid = inputs_f + attn_sum + out_bias.astype(jnp.float32)
    normed_two, norm2_back = jax.vjp(
        layer_norm, resid, ln2_gain.astype(jnp.float32), ln2_bias.astype(jnp.float32)
    )
    normed_two_low = normed_two.astype(jnp.bfloat16)
    gathered_two = lax.all_gather(normed_two_low, "tensor", axis=0, tiled=True)
    hidden = jnp.dot(gathered_two, w_fc1, preferred_element_type=jnp.float32) + fc1_bias.astype(
        jnp.float32
    )
    active, gelu_back = jax.vjp(gelu_exact, hidden)
    active_low = active.astype(jnp.bfloat16)
    branch = lax.psum_scatter(
        jnp.dot(active_low, w_fc2, preferred_element_type=jnp.float32).astype(jnp.bfloat16),
        "tensor",
        scatter_dimension=0,
        tiled=True,
    ).astype(jnp.float32)
    output_f = resid + branch + fc2_bias.astype(jnp.float32)
    output = output_f.astype(jnp.bfloat16)
    out_values = output.astype(jnp.float32)
    first_col = first_rows[:, None]
    moment_one, moment_two, cls_count = lax.psum(
        (
            jnp.sum(first_col * out_values, axis=0),
            jnp.sum(first_col * out_values * out_values, axis=0),
            jnp.sum(first_rows),
        ),
        ("dp", "tensor"),
    )
    cls_mean = moment_one / cls_count
    cls_spread = moment_two / cls_count - cls_mean * cls_mean
    cls_features = first_col * (out_values - cls_mean) * lax.rsqrt(cls_spread + 1e-05)
    grad_out = cotangent.astype(jnp.float32) * live_rows[:, None]
    grad_fc2_bias = jnp.sum(grad_out, axis=0)
    grad_branch = grad_out.astype(jnp.bfloat16)
    grad_rows = lax.all_gather(grad_branch, "tensor", axis=0, tiled=True)
    grad_fc2 = jnp.einsum("ni,nj->ij", active_low, grad_rows, preferred_element_type=jnp.float32)
    grad_active = jnp.dot(grad_rows, w_fc2.T, preferred_element_type=jnp.float32)
    grad_hidden = gelu_back(grad_active)[0].astype(jnp.bfloat16)
    grad_fc1 = jnp.einsum(
        "ni,nj->ij", gathered_two, grad_hidden, preferred_element_type=jnp.float32
    )
    grad_fc1_bias = place_block(
        jnp.sum(grad_hidden.astype(jnp.float32), axis=0), tensor_index, tensor_parts
    )
    grad_normed_two = lax.psum_scatter(
        jnp.dot(grad_hidden, w_fc1.T, preferred_element_type=jnp.float32).astype(jnp.bfloat16),
        "tensor",
        scatter_dimension=0,
        tiled=True,
    ).astype(jnp.float32)
    grad_resid_norm, grad_ln2_gain, grad_ln2_bias = norm2_back(grad_normed_two)
    grad_resid = grad_out + grad_resid_norm
    grad_out_bias = jnp.sum(grad_resid, axis=0)
    grad_attn = grad_resid.astype(jnp.bfloat16)
    attn_rows = lax.all_gather(grad_attn, "tensor", axis=0, tiled=True)
    grad_w_out = jnp.einsum("ni,nj->ij", heads_out, attn_rows, preferred_element_type=jnp.float32)
    grad_heads = jnp.dot(attn_rows, weight_out.T, preferred_element_type=jnp.float32).astype(
        jnp.bfloat16
    )
    grad_queries, grad_keys, grad_values = lax.map(
        partial(block_backward, score_scale=score_scale),
        (
            blocked(query_rows),
            blocked(key_rows),
            blocked(value_rows),
            label_blocks,
            log_totals,
            blocked(grad_heads),
        ),
    )
    grad_queries = grad_queries.reshape(attn_total, head_count, HD)
    grad_keys = grad_keys.reshape(attn_total, head_count, HD)
    grad_values = grad_values.reshape(attn_total, head_count, HD)
    grad_mixed = jnp.stack([grad_queries, grad_keys, grad_values], axis=2).reshape(
        attn_total, head_count * 3 * HD
    )
    query_sums = jnp.sum(grad_queries.astype(jnp.float32), axis=0).reshape(-1)
    value_sums = jnp.sum(grad_values.astype(jnp.float32), axis=0).reshape(-1)
    grad_w_qkv = jnp.einsum(
        "ni,nj->ij", attn_source, grad_mixed, preferred_element_type=jnp.float32
    )
    grad_q_bias = place_block(query_sums, tensor_index, tensor_parts)
    grad_v_bias = place_block(value_sums, tensor_index, tensor_parts)
    grad_normed = lax.psum_scatter(
        jnp.dot(grad_mixed, weight_qkv.T, preferred_element_type=jnp.float32).astype(jnp.bfloat16),
        "tensor",
        scatter_dimension=0,
        tiled=True,
    ).astype(jnp.float32)
    grad_inputs_norm, grad_ln1_gain, grad_ln1_bias = norm1_back(grad_normed)
    grad_tokens = (grad_resid + grad_inputs_norm).astype(jnp.bfloat16)
    sum_qkv, sum_out, sum_fc1, sum_fc2 = (
        lax.psum_scatter(grad_w_qkv, "dp", scatter_dimension=0, tiled=True),
        lax.psum_scatter(grad_w_out, "dp", scatter_dimension=1, tiled=True),
        lax.psum_scatter(grad_fc1, "dp", scatter_dimension=0, tiled=True),
        lax.psum_scatter(grad_fc2, "dp", scatter_dimension=1, tiled=True),
    )
    small_sums = lax.psum(
        (
            grad_ln1_gain,
            grad_ln1_bias,
            grad_q_bias,
            grad_v_bias,
            grad_out_bias,
            grad_fc1_bias,
            grad_fc2_bias,
            grad_ln2_gain,
            grad_ln2_bias,
        ),
        ("dp", "tensor"),
    )
    return (
        output,
        grad_tokens,
        cls_features,
        sum_qkv,
        small_sums[2],
        small_sums[3],
        sum_out,
        small_sums[4],
        sum_fc1,
        small_sums[5],
        sum_fc2,
        small_sums[6],
        small_sums[0],
        small_sums[1],
        small_sums[7],
        small_sums[8],
    )


def solution(mesh):
    in_specs = (
        P(("dp", "tensor"), None),
        P("dp"),
        P(("dp", "tensor"), None),
        P(),
        P(),
        P(None, "tensor"),
        P("tensor"),
        P("tensor"),
        P("tensor", None),
        P(),
        P(),
        P(),
        P(None, "tensor"),
        P("tensor"),
        P("tensor", None),
        P(),
    )
    out_specs = (
        P(("dp", "tensor"), None),
        P(("dp", "tensor"), None),
        P(("dp", "tensor"), None),
        P("dp", "tensor"),
        P(),
        P(),
        P("tensor", "dp"),
        P(),
        P("dp", "tensor"),
        P(),
        P("tensor", "dp"),
        P(),
        P(),
        P(),
        P(),
        P(),
    )
    return jax.shard_map(
        on_device, mesh=mesh, in_specs=in_specs, out_specs=out_specs, check_vma=False
    )
```

profile of v0, /device:TPU:0, one launch (start us, length us, event | category | flops | bytes accessed | tf_op | source)
XLA Modules:
  0.0 796.6 jit_solution(3495754331182693921)
XLA Ops:
  14.8 66.1 %all-gather.5.cloned.1.call-done = bf16[2048,768]{1,0:T(8,128)(2,1)} async-done(((bf16[512,768]{1,0:T(8,128)(2,1)}), bf16[2048,768]{1,0:T(8,128)(2,1)}) %all-gather.5.cloned.1.call-update) | async-done | bytes 3145744 | tf_op jit(solution)/shard_map/all_gather | solution.py:108
  98.2 20.1 %while.26 = (s32[]{:T(128)}, bf16[4,512,3,64]{1,3,2,0:T(8,128)(2,1)}, f32[4,3,512]{2,1,0:T(4,128)}, bf16[4,512,3,64]{1,3,2,0:T(8,128)(2,1)}, s32[4,512]{1,0:T(4,...) while((s32[]{:T(128)}, ...), condition=%wide.region_5.6_spmd, body=%wide.region_2.5_spmd.sunk | while | flops 211122688 | bytes 11332185 | solution.py:127
  125.5 57.9 %reduce-scatter.11.cloned.1.call-done = bf16[512,768]{1,0:T(8,128)(2,1)} async-done(((bf16[2048,768]{1,0:T(8,128)(2,1)}), bf16[512,768]{1,0:T(8,128)(2,1)}) %reduce-scatter.11.cloned.1.call-update) | async-done | bytes 786448 | tf_op jit(solution)/shard_map/reduce_scatter | solution.py:132
  195.3 57.2 %all-gather.7.cloned.1.call-done = bf16[2048,768]{1,0:T(8,128)(2,1)} async-done(((bf16[512,768]{1,0:T(8,128)(2,1)}), bf16[2048,768]{1,0:T(8,128)(2,1)}) %all-gather.7.cloned.1.call-update) | async-done | bytes 3145744 | tf_op jit(solution)/shard_map/all_gather | solution.py:143
  252.5 7.5 fusion.98
  260.0 56.6 %all-gather.9.cloned.1.call-done = bf16[2048,768]{1,0:T(8,128)(2,1)} async-done(((bf16[512,768]{1,0:T(8,128)(2,1)}), bf16[2048,768]{1,0:T(8,128)(2,1)}) %all-gather.9.cloned.1.call-update) | async-done | bytes 3145744 | tf_op jit(solution)/shard_map/all_gather | solution.py:173
  316.6 20.2 %convert_reduce_fusion = (f32[768]{0:T(1024)}, bf16[2048,768]{1,0:T(8,128)(2,1)S(1)}, f32[2048,768]{1,0:T(8,128)}) fusion(f32[2048,768]{1,0:T(8,128)} %fusion.98, f32[768]{0:T(1024)} %convert_element_type.159, bf16[2048,768]{1,0:T(8,128)(2,1)} %all-gather.9.cloned.1.call-done, bf16[768,768]{1,0:T(8,128)(2,1)S(1)} %copy-done), kind=kOutput, calls=%fused_computation.64 | convolution fusion | flops 2533883136 | bytes 20060160 | tf_op jit(solution)/shard_map/dot_general | solution.py:175
  338.5 4.0 convolution_convert_fusion
  342.6 5.5 multiply_convert_fusion.1
  349.7 4.0 convolution_convert_fusion.1
  353.8 10.8 %all-gather.11.cloned.1.call-start = ((), (), s32[]{:S(2)}) async-start(), calls=%async_computation.14 | async-start | bytes 3932160 | tf_op jit(solution)/shard_map/all_gather | solution.py:193
  364.6 37.1 %reduce-scatter.15.cloned.1.call-done = bf16[512,768]{1,0:T(8,128)(2,1)} async-done(((bf16[2048,768]{1,0:T(8,128)(2,1)}), bf16[512,768]{1,0:T(8,128)(2,1)}) %reduce-scatter.15.cloned.1.call-update) | async-done | bytes 786448 | tf_op jit(solution)/shard_map/reduce_scatter | solution.py:183
  405.9 58.3 %reduce-scatter.13.cloned.1.call-done = bf16[512,768]{1,0:T(8,128)(2,1)} async-done(((bf16[2048,768]{1,0:T(8,128)(2,1)}), bf16[512,768]{1,0:T(8,128)(2,1)}) %reduce-scatter.13.cloned.1.call-update) | async-done | bytes 786448 | tf_op jit(solution)/shard_map/reduce_scatter | solution.py:149
  469.8 63.4 %all-gather.11.cloned.1.call-done = bf16[2048,768]{1,0:T(8,128)(2,1)} async-done(((bf16[512,768]{1,0:T(8,128)(2,1)}), bf16[2048,768]{1,0:T(8,128)(2,1)}) %all-gather.11.cloned.1.call-update) | async-done | bytes 3145744 | tf_op jit(solution)/shard_map/all_gather | solution.py:193
  533.2 4.2 convolution_bitcast_fusion
  546.2 31.7 %while.27 = (s32[]{:T(128)}, bf16[4,512,3,64]{1,3,2,0:T(8,128)(2,1)}, bf16[4,512,3,64]{1,3,2,0:T(8,128)(2,1)}, bf16[4,512,3,64]{1,3,2,0:T(8,128)(2,1)}, bf16[4,5...) while((s32[]{:T(128)}, ...), condition=%wide.region_15.16_spmd, body=%wide.region_13.15_spmd.sunk | while | flops 511146496 | bytes 26127476 | solution.py:198
  589.3 4.1 convolution_convert_fusion.2
  593.7 6.9 fusion.100
  600.7 6.9 fusion.101
  607.7 6.5 fusion.99
  619.5 33.0 %reduce-scatter.17.cloned.1.call-done = bf16[512,768]{1,0:T(8,128)(2,1)} async-done(((bf16[2048,768]{1,0:T(8,128)(2,1)}), bf16[512,768]{1,0:T(8,128)(2,1)}) %reduce-scatter.17.cloned.1.call-update) | async-done | bytes 786448 | tf_op jit(solution)/shard_map/reduce_scatter | solution.py:222
  656.4 41.9 %all-reduce = (f32[768]{0:T(1024)S(1)}, f32[]{:T(128)}, f32[768]{0:T(1024)S(1)}, f32[768]{0:T(1024)}, f32[768]{0:T(1024)}, /*index=5*/f32[768]{0:T(1024)}, f32[3...) all-reduce(f32[768]{0:T(1024)S(1)} %get-tuple-element.228, ...), channel_id=1, replica_groups=mesh['dp'=8,'tensor'=4] {'dp','tensor'}, use_global_device_ids=true, to_apply=%region_24.25 | all-reduce | flops 10753 | bytes 86024 | tf_op jit(solution)/shard_map/psum | solution.py:159
  704.2 41.2 %reduce-scatter.23.cloned.1.call-done = f32[768,96]{0,1:T(8,128)} async-done(((f32[768,768]{0,1:T(8,128)}), f32[768,96]{0,1:T(8,128)}) %reduce-scatter.23.cloned.1.call-update) | async-done | bytes 294928 | tf_op jit(solution)/shard_map/reduce_scatter | solution.py:234
  745.4 44.0 %reduce-scatter.19.cloned.1.call-done = f32[96,576]{1,0:T(8,128)} async-done(((f32[768,576]{1,0:T(8,128)}), f32[96,576]{1,0:T(8,128)}) %reduce-scatter.19.cloned.1.call-update) | async-done | bytes 221200 | tf_op jit(solution)/shard_map/reduce_scatter | solution.py:231
  (255 shorter events, 144.0 us)
Async XLA Ops:
  7.2 309.5 %copy-start = (bf16[768,768]{1,0:T(8,128)(2,1)S(1)}, bf16[768,768]{1,0:T(8,128)(2,1)}, u32[]{:S(2)}) copy-start(bf16[768,768]{1,0:T(8,128)(2,1)} %param.34) | copy-start | bytes 3538948
  7.2 73.7 %copy-start.42 = (bf16[768,576]{0,1:T(8,128)(2,1)S(1)}, bf16[768,576]{0,1:T(8,128)(2,1)}, u32[]{:S(2)}) copy-start(bf16[768,576]{0,1:T(8,128)(2,1)} %param.25) | copy-start | bytes 2654212
  7.2 73.7 %all-gather.5.cloned.1.call-start = ((), (), s32[]{:S(2)}) async-start(), calls=%async_computation.8 | async-start | bytes 3932160 | tf_op jit(solution)/shard_map/all_gather | solution.py:108
  8.7 76.1 %copy-start.17 = (f32[512]{0:T(512)}, f32[512]{0:T(512)S(1)}, u32[]{:S(2)}) copy-start(f32[512]{0:T(512)S(1)} %broadcast_multiply_fusion.1) | copy-start | bytes 6148
  10.8 74.0 %copy-start.22 = (f32[512]{0:T(512)}, f32[512]{0:T(512)S(1)}, u32[]{:S(2)}) copy-start(f32[512]{0:T(512)S(1)} %fusion.90) | copy-start | bytes 6148
  11.5 73.3 %copy-start.15 = (f32[768]{0:T(1024)}, f32[768]{0:T(1024)S(1)}, u32[]{:S(2)}) copy-start(f32[768]{0:T(1024)S(1)} %convert_element_type.147) | copy-start | bytes 9220
  14.6 168.8 %reduce-scatter.11.cloned.1.call-start = ((), (), s32[]{:S(2)}) async-start(), calls=%async_computation.9 | async-start | bytes 3932160 | tf_op jit(solution)/shard_map/reduce_scatter | solution.py:132
  124.1 128.4 %all-gather.7.cloned.1.call-start = ((), (), s32[]{:S(2)}) async-start(), calls=%async_computation.10 | async-start | bytes 3932160 | tf_op jit(solution)/shard_map/all_gather | solution.py:143
  189.0 127.6 %all-gather.9.cloned.1.call-start = ((), (), s32[]{:S(2)}) async-start(), calls=%async_computation.12 | async-start | bytes 3932160 | tf_op jit(solution)/shard_map/all_gather | solution.py:173
  194.0 207.7 %reduce-scatter.15.cloned.1.call-start = ((), (), s32[]{:S(2)}) async-start(), calls=%async_computation.13 | async-start | bytes 3932160 | tf_op jit(solution)/shard_map/reduce_scatter | solution.py:183
  342.5 121.7 %reduce-scatter.13.cloned.1.call-start = ((), (), s32[]{:S(2)}) async-start(), calls=%async_computation.11 | async-start | bytes 3932160 | tf_op jit(solution)/shard_map/reduce_scatter | solution.py:149
  353.7 110.5 %copy-start.27 = (f32[512]{0:T(512)S(1)}, f32[512]{0:T(512)}, u32[]{:S(2)}) copy-start(f32[512]{0:T(512)} %copy-done.26) | copy-start | bytes 6148
  353.8 110.5 %copy-start.32 = (f32[512]{0:T(512)S(1)}, f32[512]{0:T(512)}, u32[]{:S(2)}) copy-start(f32[512]{0:T(512)} %get-tuple-element.219) | copy-start | bytes 6148
  353.8 179.5 %all-gather.11.cloned.1.call-start = ((), (), s32[]{:S(2)}) async-start(), calls=%async_computation.14 | async-start | bytes 3932160 | tf_op jit(solution)/shard_map/all_gather | solution.py:193
  401.7 62.5 %copy-start.8 = (bf16[512,768]{1,0:T(8,128)(2,1)S(1)}, bf16[512,768]{1,0:T(8,128)(2,1)}, u32[]{:S(2)}) copy-start(bf16[512,768]{1,0:T(8,128)(2,1)} %reduce-scatter.15.cloned.1.call-done) | copy-start | bytes 2359300
  467.6 65.6 %copy-start.10 = (bf16[24,8,4,512]{3,1,2,0:T(8,128)(2,1)S(1)}, bf16[24,8,4,512]{3,1,2,0:T(8,128)(2,1)}, u32[]{:S(2)}) copy-start(bf16[24,8,4,512]{3,1,2,0:T(8,128)(2,1)} %copy-done.9) | copy-start | bytes 2359300
  469.7 148.2 %reduce-scatter.25.cloned.1.call-start = ((), (), s32[]{:S(2)}) async-start(), calls=%async_computation.19 | async-start | bytes 884736
  469.8 67.7 %copy-start.14 = (bf16[192,768]{1,0:T(8,128)(2,1)S(1)}, bf16[192,768]{1,0:T(8,128)(2,1)}, u32[]{:S(2)}) copy-start(bf16[192,768]{1,0:T(8,128)(2,1)} %param.28) | copy-start | bytes 884740
  537.4 115.2 %reduce-scatter.17.cloned.1.call-start = ((), (), s32[]{:S(2)}) async-start(), calls=%async_computation.15 | async-start | bytes 3932160 | tf_op jit(solution)/shard_map/reduce_scatter | solution.py:222
  593.4 110.8 %reduce-scatter.21.cloned.1.call-start = ((), (), s32[]{:S(2)}) async-start(), calls=%async_computation.17 | async-start | bytes 2654208 | tf_op jit(solution)/shard_map/reduce_scatter | solution.py:233
  600.6 144.8 %reduce-scatter.23.cloned.1.call-start = ((), (), s32[]{:S(2)}) async-start(), calls=%async_computation.18 | async-start | bytes 2654208 | tf_op jit(solution)/shard_map/reduce_scatter | solution.py:234
  607.6 181.8 %reduce-scatter.19.cloned.1.call-start = ((), (), s32[]{:S(2)}) async-start(), calls=%async_computation.16 | async-start | bytes 2211840 | tf_op jit(solution)/shard_map/reduce_scatter | solution.py:231
  616.0 85.6 %copy-start.5 = (f32[512,768]{1,0:T(8,128)S(1)}, f32[512,768]{1,0:T(8,128)}, u32[]{:S(2)}) copy-start(f32[512,768]{1,0:T(8,128)} %copy-done.4) | copy-start | bytes 4718596
  698.9 90.5 %copy-start.1 = (bf16[768,768]{1,0:T(8,128)(2,1)S(1)}, bf16[768,768]{1,0:T(8,128)(2,1)}, u32[]{:S(2)}) copy-start(bf16[768,768]{1,0:T(8,128)(2,1)} %param.34) | copy-start | bytes 3538948
  (33 other events, 464.5 us)
Sparse Core Ops, SparseCore 0:
  14.7 66.1 all-gather.4
  124.3 59.0 reduce-scatter.10
  189.1 63.3 all-gather.6
  254.5 62.0 all-gather.8
  342.6 59.0 reduce-scatter.14
  403.9 60.3 reduce-scatter.12
  469.8 63.3 all-gather.10
  537.5 33.5 reduce-scatter.24
  593.5 59.0 reduce-scatter.16
  656.4 42.6 reduce-scatter.20
  703.0 42.3 reduce-scatter.22
  749.2 40.1 reduce-scatter.18
where the time goes:
time: 806 us; the launch traced here: 797 us
  waiting for transfers between devices  515 us (64%)
  matrix products  112 us (14%)
  other arithmetic  57.9 us (7%)
  local copies, waits for them, and re-layouts  42.5 us (5%)
  blocking collectives  41.9 us (5%)
  between operations  15.1 us (2%)
  starting transfers between devices  11.8 us (1%)
    all_gather x1, waiting for transfers between devices, on_device(): attn_source = lax.all_gather(normed_low, 'tensor', axis=0, tiled=True)  66.1 us
    all_gather x1, waiting for transfers between devices, on_device(): attn_rows = lax.all_gather(grad_attn, 'tensor', axis=0, tiled=True)  63.4 us
    reduce_scatter x1, waiting for transfers between devices, on_device(): lax.psum_scatter(jnp.dot(active_low, w_fc2, preferred_element_type=jnp.fl...  58.3 us
    reduce_scatter x1, waiting for transfers between devices, on_device(): lax.psum_scatter(jnp.dot(heads_out, weight_out, preferred_element_type=jn...  57.9 us
    all_gather x1, waiting for transfers between devices, on_device(): gathered_two = lax.all_gather(normed_two_low, 'tensor', axis=0, tiled=True)  57.2 us
    all_gather x1, waiting for transfers between devices, on_device(): grad_rows = lax.all_gather(grad_branch, 'tensor', axis=0, tiled=True)  56.6 us
    reduce_scatter x1, waiting for transfers between devices, on_device(): lax.psum_scatter(grad_w_qkv, 'dp', scatter_dimension=0, tiled=True)  44 us
    psum x1, blocking collectives, on_device(): lax.psum((jnp.sum(first_col * out_values, axis=0), jnp.sum(first_col * ou...  41.9 us
  transfers between devices with their start and end apart: 12, of which 10 were waited for; matrix products, arithmetic and copies ran while one was open for 15% of the time, Pallas kernels for 0%

commit v1 on v0

--- a/solution.py
+++ b/solution.py
@@ -7,6 +7,27 @@
 
 HD = 64
 SEQ = 512
+
+
+def collect(shard, axis, dim):
+    size, index, rows = (lax.axis_size(axis), lax.axis_index(axis), shard.shape[dim])
+    ahead = [(i, (i + 1) % size) for i in range(size)]
+    behind = [(i, (i - 1) % size) for i in range(size)]
+    out = jnp.zeros((*shard.shape[:dim], size * rows, *shard.shape[dim + 1 :]), shard.dtype)
+    out = lax.dynamic_update_slice_in_dim(out, shard, index * rows, axis=dim)
+    from_left = from_right = shard
+    halfway = size // 2
+    for turn in range(1, halfway + 1):
+        from_left = lax.ppermute(from_left, axis, ahead)
+        out = lax.dynamic_update_slice_in_dim(
+            out, from_left, (index - turn) % size * rows, axis=dim
+        )
+        if turn < size - halfway:
+            from_right = lax.ppermute(from_right, axis, behind)
+            out = lax.dynamic_update_slice_in_dim(
+                out, from_right, (index + turn) % size * rows, axis=dim
+            )
+    return out
 
 
 def layer_norm(values, gain, shift):
@@ -140,7 +161,7 @@
         layer_norm, resid, ln2_gain.astype(jnp.float32), ln2_bias.astype(jnp.float32)
     )
     normed_two_low = normed_two.astype(jnp.bfloat16)
-    gathered_two = lax.all_gather(normed_two_low, "tensor", axis=0, tiled=True)
+    gathered_two = collect(normed_two_low, "tensor", 0)
     hidden = jnp.dot(gathered_two, w_fc1, preferred_element_type=jnp.float32) + fc1_bias.astype(
         jnp.float32
     )

time: 806 us -> 795 us (0.986)
  waiting for transfers between devices: 515 us -> 460 us
  starting transfers between devices: 11.8 us -> 47.4 us
    ppermute x0 -> x3, waiting for transfers between devices: none -> 62.5 us  [the longest x2 62.4 us: collect(): from_left = lax.ppermute(from_left, axis, ahead)]
    all_gather x1 -> x0, waiting for transfers between devices: 57.2 us -> none  [on_device(): gathered_two = lax.all_gather(normed_two_low, 'tensor', axis=0, tiled=True)]
    all_gather x1, waiting for transfers between devices: 56.6 us -> 0.01 us  [on_device(): grad_rows = lax.all_gather(grad_branch, 'tensor', axis=0, tiled=True)]
    ppermute x0 -> x3, starting transfers between devices: none -> 35.7 us  [the longest x2 32.7 us: collect(): from_left = lax.ppermute(from_left, axis, ahead)]
  transfers between devices with their start and end apart: 12 -> 14, of which waited for: 10 -> 10; matrix products, arithmetic and copies ran while one was open for 15% -> 17% of each run, Pallas kernels for 0% -> 0%
where the time goes in v1:
time: 795 us; the launch traced here: 785 us
  waiting for transfers between devices  460 us (58%)
  matrix products  112 us (14%)
  other arithmetic  58.4 us (7%)
  local copies, waits for them, and re-layouts  50.4 us (6%)
  starting transfers between devices  47.4 us (6%)
  blocking collectives  41.8 us (5%)
  between operations  14.8 us (2%)
    all_gather x1, waiting for transfers between devices, on_device(): attn_source = lax.all_gather(normed_low, 'tensor', axis=0, tiled=True)  64.9 us
    all_gather x1, waiting for transfers between devices, on_device(): attn_rows = lax.all_gather(grad_attn, 'tensor', axis=0, tiled=True)  63.4 us
    ppermute x2, waiting for transfers between devices, collect(): from_left = lax.ppermute(from_left, axis, ahead)  62.4 us
    reduce_scatter x1, waiting for transfers between devices, on_device(): lax.psum_scatter(jnp.dot(active_low, w_fc2, preferred_element_type=jnp.fl...  58.3 us
    reduce_scatter x1, waiting for transfers between devices, on_device(): lax.psum_scatter(jnp.dot(heads_out, weight_out, preferred_element_type=jn...  53.7 us
    reduce_scatter x1, waiting for transfers between devices, on_device(): lax.psum_scatter(grad_w_qkv, 'dp', scatter_dimension=0, tiled=True)  44.2 us
    psum x1, blocking collectives, on_device(): lax.psum((jnp.sum(first_col * out_values, axis=0), jnp.sum(first_col * ou...  41.8 us
    reduce_scatter x1, waiting for transfers between devices, on_device(): lax.psum_scatter(grad_fc2, 'dp', scatter_dimension=1, tiled=True)  41.2 us
  transfers between devices with their start and end apart: 14, of which 10 were waited for; matrix products, arithmetic and copies ran while one was open for 17% of the time, Pallas kernels for 0%

profile of v1, /device:TPU:0, one launch (start us, length us, event | category | flops | bytes accessed | tf_op | source)
XLA Modules:
  0.0 784.9 jit_solution(18319248191558617697)
XLA Ops:
  16.0 64.9 %all-gather.4.cloned.1.call-done = bf16[2048,768]{1,0:T(8,128)(2,1)} async-done(((bf16[512,768]{1,0:T(8,128)(2,1)}), bf16[2048,768]{1,0:T(8,128)(2,1)}) %all-gather.4.cloned.1.call-update) | async-done | bytes 3145744 | tf_op jit(solution)/shard_map/all_gather | solution.py:129
  98.2 20.1 %while.26 = (s32[]{:T(128)}, bf16[4,512,3,64]{1,3,2,0:T(8,128)(2,1)}, f32[4,3,512]{2,1,0:T(4,128)}, bf16[4,512,3,64]{1,3,2,0:T(8,128)(2,1)}, s32[4,512]{1,0:T(4,...) while((s32[]{:T(128)}, ...), condition=%wide.region_5.6_spmd, body=%wide.region_2.5_spmd.sunk | while | flops 211122688 | bytes 11332185 | solution.py:148
  129.6 53.7 %reduce-scatter.11.cloned.1.call-done = bf16[512,768]{1,0:T(8,128)(2,1)} async-done(((bf16[2048,768]{1,0:T(8,128)(2,1)}), bf16[512,768]{1,0:T(8,128)(2,1)}) %reduce-scatter.11.cloned.1.call-update) | async-done | bytes 786448 | tf_op jit(solution)/shard_map/reduce_scatter | solution.py:153
  194.5 33.9 %collective-permute-done = bf16[512,768]{1,0:T(8,128)(2,1)} collective-permute-done((bf16[512,768]{1,0:T(8,128)(2,1)}, bf16[512,768]{1,0:T(8,128)(2,1)}, u32[]{:S(2)}, u32[]{:S(2)}) %collective-permute-start) | collective-permute-done | bytes 786464 | tf_op jit(solution)/shard_map/ppermute | solution.py:21
  228.5 31.8 %collective-permute-start.2 = (bf16[512,768]{1,0:T(8,128)(2,1)}, bf16[512,768]{1,0:T(8,128)(2,1)}, u32[]{:S(2)}, u32[]{:S(2)}) collective-permute-start(bf16[512,768]{1,0:T(8,128)(2,1)} %collective-permute-done), channel_id=1, source_target_pairs={{0,1},{1,2},{2,3},{3,0},{4,5},{5,6},{6,7},{7,4},{8,9},{9,10},{10,1... | collective-permute-start | bytes 2359304 | tf_op jit(solution)/shard_map/ppermute | solution.py:21
  265.8 28.5 %collective-permute-done.2 = bf16[512,768]{1,0:T(8,128)(2,1)} collective-permute-done((bf16[512,768]{1,0:T(8,128)(2,1)}, bf16[512,768]{1,0:T(8,128)(2,1)}, u32[]{:S(2)}, u32[]{:S(2)}) %collective-permute-start.2) | collective-permute-done | bytes 786464 | tf_op jit(solution)/shard_map/ppermute | solution.py:21
  296.4 7.2 fusion.98
  303.6 20.2 %convert_reduce_fusion = (f32[768]{0:T(1024)}, bf16[2048,768]{1,0:T(8,128)(2,1)S(1)}, f32[2048,768]{1,0:T(8,128)}) fusion(f32[2048,768]{1,0:T(8,128)} %fusion.98, f32[768]{0:T(1024)} %convert_element_type.159, bf16[2048,768]{1,0:T(8,128)(2,1)} %all-gather.6.cloned.1.call-done, bf16[768,768]{1,0:T(8,128)(2,1)S(1)} %copy-done), kind=kOutput, calls=%fused_computation.64 | convolution fusion | flops 2533883136 | bytes 20060160 | tf_op jit(solution)/shard_map/dot_general | solution.py:196
  325.5 4.0 convolution_convert_fusion
  329.6 5.5 multiply_convert_fusion.1
  340.8 10.8 %all-gather.8.cloned.1.call-start = ((), (), s32[]{:S(2)}) async-start(), calls=%async_computation.13 | async-start | bytes 3932160 | tf_op jit(solution)/shard_map/all_gather | solution.py:214
  351.6 38.5 %reduce-scatter.15.cloned.1.call-done = bf16[512,768]{1,0:T(8,128)(2,1)} async-done(((bf16[2048,768]{1,0:T(8,128)(2,1)}), bf16[512,768]{1,0:T(8,128)(2,1)}) %reduce-scatter.15.cloned.1.call-update) | async-done | bytes 786448 | tf_op jit(solution)/shard_map/reduce_scatter | solution.py:204
  394.3 58.3 %reduce-scatter.13.cloned.1.call-done = bf16[512,768]{1,0:T(8,128)(2,1)} async-done(((bf16[2048,768]{1,0:T(8,128)(2,1)}), bf16[512,768]{1,0:T(8,128)(2,1)}) %reduce-scatter.13.cloned.1.call-update) | async-done | bytes 786448 | tf_op jit(solution)/shard_map/reduce_scatter | solution.py:170
  458.3 63.4 %all-gather.8.cloned.1.call-done = bf16[2048,768]{1,0:T(8,128)(2,1)} async-done(((bf16[512,768]{1,0:T(8,128)(2,1)}), bf16[2048,768]{1,0:T(8,128)(2,1)}) %all-gather.8.cloned.1.call-update) | async-done | bytes 3145744 | tf_op jit(solution)/shard_map/all_gather | solution.py:214
  521.7 4.1 convolution_bitcast_fusion
  534.6 31.7 %while.27 = (s32[]{:T(128)}, bf16[4,512,3,64]{1,3,2,0:T(8,128)(2,1)}, bf16[4,512,3,64]{1,3,2,0:T(8,128)(2,1)}, bf16[4,512,3,64]{1,3,2,0:T(8,128)(2,1)}, bf16[4,5...) while((s32[]{:T(128)}, ...), condition=%wide.region_15.16_spmd, body=%wide.region_13.15_spmd.sunk | while | flops 511146496 | bytes 26127476 | solution.py:219
  577.7 4.1 convolution_convert_fusion.2
  582.1 7.0 fusion.100
  589.1 6.9 fusion.101
  596.1 6.5 fusion.99
  608.0 33.0 %reduce-scatter.17.cloned.1.call-done = bf16[512,768]{1,0:T(8,128)(2,1)} async-done(((bf16[2048,768]{1,0:T(8,128)(2,1)}), bf16[512,768]{1,0:T(8,128)(2,1)}) %reduce-scatter.17.cloned.1.call-update) | async-done | bytes 786448 | tf_op jit(solution)/shard_map/reduce_scatter | solution.py:243
  644.8 41.8 %all-reduce = (f32[768]{0:T(1024)S(1)}, f32[]{:T(128)}, f32[768]{0:T(1024)S(1)}, f32[768]{0:T(1024)}, f32[768]{0:T(1024)}, /*index=5*/f32[768]{0:T(1024)}, f32[3...) all-reduce(f32[768]{0:T(1024)S(1)} %get-tuple-element.230, ...), channel_id=1, replica_groups=mesh['dp'=8,'tensor'=4] {'dp','tensor'}, use_global_device_ids=true, to_apply=%region_24.25 | all-reduce | flops 10753 | bytes 86024 | tf_op jit(solution)/shard_map/psum | solution.py:180
  692.6 41.2 %reduce-scatter.23.cloned.1.call-done = f32[768,96]{0,1:T(8,128)} async-done(((f32[768,768]{0,1:T(8,128)}), f32[768,96]{0,1:T(8,128)}) %reduce-scatter.23.cloned.1.call-update) | async-done | bytes 294928 | tf_op jit(solution)/shard_map/reduce_scatter | solution.py:255
  733.8 44.2 %reduce-scatter.19.cloned.1.call-done = f32[96,576]{1,0:T(8,128)} async-done(((f32[768,576]{1,0:T(8,128)}), f32[96,576]{1,0:T(8,128)}) %reduce-scatter.19.cloned.1.call-update) | async-done | bytes 221200 | tf_op jit(solution)/shard_map/reduce_scatter | solution.py:252
  (260 shorter events, 160.2 us)
Async XLA Ops:
  7.2 296.4 %copy-start = (bf16[768,768]{1,0:T(8,128)(2,1)S(1)}, bf16[768,768]{1,0:T(8,128)(2,1)}, u32[]{:S(2)}) copy-start(bf16[768,768]{1,0:T(8,128)(2,1)} %param.34) | copy-start | bytes 3538948
  7.2 73.7 %copy-start.41 = (bf16[768,576]{0,1:T(8,128)(2,1)S(1)}, bf16[768,576]{0,1:T(8,128)(2,1)}, u32[]{:S(2)}) copy-start(bf16[768,576]{0,1:T(8,128)(2,1)} %param.25) | copy-start | bytes 2654212
  7.2 73.7 %all-gather.4.cloned.1.call-start = ((), (), s32[]{:S(2)}) async-start(), calls=%async_computation.8 | async-start | bytes 3932160 | tf_op jit(solution)/shard_map/all_gather | solution.py:129
  8.7 76.1 %copy-start.18 = (f32[512]{0:T(512)}, f32[512]{0:T(512)S(1)}, u32[]{:S(2)}) copy-start(f32[512]{0:T(512)S(1)} %broadcast_multiply_fusion.1) | copy-start | bytes 6148
  10.8 74.0 %copy-start.23 = (f32[512]{0:T(512)}, f32[512]{0:T(512)S(1)}, u32[]{:S(2)}) copy-start(f32[512]{0:T(512)S(1)} %fusion.90) | copy-start | bytes 6148
  11.5 73.3 %copy-start.16 = (f32[768]{0:T(1024)}, f32[768]{0:T(1024)S(1)}, u32[]{:S(2)}) copy-start(f32[768]{0:T(1024)S(1)} %convert_element_type.147) | copy-start | bytes 9220
  14.6 168.7 %reduce-scatter.11.cloned.1.call-start = ((), (), s32[]{:S(2)}) async-start(), calls=%async_computation.9 | async-start | bytes 3932160 | tf_op jit(solution)/shard_map/reduce_scatter | solution.py:153
  124.1 179.5 %all-gather.6.cloned.1.call-start = ((), (), s32[]{:S(2)}) async-start(), calls=%async_computation.11 | async-start | bytes 3932160 | tf_op jit(solution)/shard_map/all_gather | solution.py:194
  126.7 263.5 %reduce-scatter.15.cloned.1.call-start = ((), (), s32[]{:S(2)}) async-start(), calls=%async_computation.12 | async-start | bytes 3932160 | tf_op jit(solution)/shard_map/reduce_scatter | solution.py:204
  190.7 37.8 %collective-permute-start = (bf16[512,768]{1,0:T(8,128)(2,1)}, bf16[512,768]{1,0:T(8,128)(2,1)}, u32[]{:S(2)}, u32[]{:S(2)}) collective-permute-start(bf16[512,768]{1,0:T(8,128)(2,1)} %get-tuple-element.223), channel_id=1, source_target_pairs={{0,1},{1,2},{2,3},{3,0},{4,5},{5,6},{6,7},{7,4},{8,9},{9,10},{10,1... | collective-permute-start | bytes 2359304 | tf_op jit(solution)/shard_map/ppermute | solution.py:21
  191.5 72.2 %collective-permute-start.1 = (bf16[512,768]{1,0:T(8,128)(2,1)}, bf16[512,768]{1,0:T(8,128)(2,1)}, u32[]{:S(2)}, u32[]{:S(2)}) collective-permute-start(bf16[512,768]{1,0:T(8,128)(2,1)} %get-tuple-element.223), channel_id=1, source_target_pairs={{0,3},{1,0},{2,1},{3,2},{4,7},{5,4},{6,5},{7,6},{8,11},{9,8},{10,9... | collective-permute-start | bytes 2359304 | tf_op jit(solution)/shard_map/ppermute | solution.py:26
  228.5 65.9 %collective-permute-start.2 = (bf16[512,768]{1,0:T(8,128)(2,1)}, bf16[512,768]{1,0:T(8,128)(2,1)}, u32[]{:S(2)}, u32[]{:S(2)}) collective-permute-start(bf16[512,768]{1,0:T(8,128)(2,1)} %collective-permute-done), channel_id=1, source_target_pairs={{0,1},{1,2},{2,3},{3,0},{4,5},{5,6},{6,7},{7,4},{8,9},{9,10},{10,1... | collective-permute-start | bytes 2359304 | tf_op jit(solution)/shard_map/ppermute | solution.py:21
  329.5 123.1 %reduce-scatter.13.cloned.1.call-start = ((), (), s32[]{:S(2)}) async-start(), calls=%async_computation.10 | async-start | bytes 3932160 | tf_op jit(solution)/shard_map/reduce_scatter | solution.py:170
  340.7 111.9 %copy-start.28 = (f32[512]{0:T(512)S(1)}, f32[512]{0:T(512)}, u32[]{:S(2)}) copy-start(f32[512]{0:T(512)} %copy-done.27) | copy-start | bytes 6148
  340.8 111.9 %copy-start.33 = (f32[512]{0:T(512)S(1)}, f32[512]{0:T(512)}, u32[]{:S(2)}) copy-start(f32[512]{0:T(512)} %get-tuple-element.219) | copy-start | bytes 6148
  340.8 180.9 %all-gather.8.cloned.1.call-start = ((), (), s32[]{:S(2)}) async-start(), calls=%async_computation.13 | async-start | bytes 3932160 | tf_op jit(solution)/shard_map/all_gather | solution.py:214
  458.2 148.2 %reduce-scatter.25.cloned.1.call-start = ((), (), s32[]{:S(2)}) async-start(), calls=%async_computation.18 | async-start | bytes 884736
  458.2 67.6 %copy-start.15 = (bf16[192,768]{1,0:T(8,128)(2,1)S(1)}, bf16[192,768]{1,0:T(8,128)(2,1)}, u32[]{:S(2)}) copy-start(bf16[192,768]{1,0:T(8,128)(2,1)} %param.28) | copy-start | bytes 884740
  525.8 115.1 %reduce-scatter.17.cloned.1.call-start = ((), (), s32[]{:S(2)}) async-start(), calls=%async_computation.14 | async-start | bytes 3932160 | tf_op jit(solution)/shard_map/reduce_scatter | solution.py:243
  581.8 110.7 %reduce-scatter.21.cloned.1.call-start = ((), (), s32[]{:S(2)}) async-start(), calls=%async_computation.16 | async-start | bytes 2654208 | tf_op jit(solution)/shard_map/reduce_scatter | solution.py:254
  589.1 144.7 %reduce-scatter.23.cloned.1.call-start = ((), (), s32[]{:S(2)}) async-start(), calls=%async_computation.17 | async-start | bytes 2654208 | tf_op jit(solution)/shard_map/reduce_scatter | solution.py:255
  596.1 181.9 %reduce-scatter.19.cloned.1.call-start = ((), (), s32[]{:S(2)}) async-start(), calls=%async_computation.15 | async-start | bytes 2211840 | tf_op jit(solution)/shard_map/reduce_scatter | solution.py:252
  604.5 85.5 %copy-start.5 = (f32[512,768]{1,0:T(8,128)S(1)}, f32[512,768]{1,0:T(8,128)}, u32[]{:S(2)}) copy-start(f32[512,768]{1,0:T(8,128)} %copy-done.4) | copy-start | bytes 4718596
  687.3 90.7 %copy-start.1 = (bf16[768,768]{1,0:T(8,128)(2,1)S(1)}, bf16[768,768]{1,0:T(8,128)(2,1)}, u32[]{:S(2)}) copy-start(bf16[768,768]{1,0:T(8,128)(2,1)} %param.34) | copy-start | bytes 3538948
  (34 other events, 642.6 us)
Sparse Core Ops, SparseCore 0:
  14.7 66.1 all-gather.3
  124.2 59.0 reduce-scatter.10
  185.5 110.6 all-gather.5
  329.6 60.4 reduce-scatter.14
  392.3 60.3 reduce-scatter.12
  458.3 63.3 all-gather.7
  526.0 33.5 reduce-scatter.24
  581.9 59.0 reduce-scatter.16
  644.9 42.6 reduce-scatter.20
  691.4 42.3 reduce-scatter.22
  737.8 40.1 reduce-scatter.18
